TPU v7x, 512 devices: a whole 4x4x16 slice. The times are simulated.
512 devices in a mesh: gx: 8 (over y, core), gy: 16 (over z), gz: 4 (over x).
Axes of the slice: x: 4, y: 4, z: 16, core: 2. Of those that a mesh axis runs over, the one named last changes fastest.
Arguments:
- source_term: float32 [32, 32, 128, 512], P(None, 'gx', 'gy', 'gz'), may hold values from -16 to 16
- labels: int32 [32, 128, 512], P('gx', 'gy', 'gz'), may hold values from 0 to 5
- conductivity_table: float32 [6], replicated, may hold values from 0.05 to 1
- send_map: int32 [8, 16, 4, 256], P('gx', 'gy', 'gz'), may hold values from -1 to 4095, as said below
- owner_slots: int32 [65536], P(('gx', 'gy', 'gz')), may hold values from 0 to 255, as said below
- sensor_data: float32 [32, 128], replicated, may hold values from -6 to 6
Outputs:
- projections: float32 [3, 128, 65536], P(None, None, ('gx', 'gy', 'gz'))
- gram_blocks: float32 [6, 65536], P(None, ('gx', 'gy', 'gz'))
Inputs may be any that keep to these rules, and one draw needn't show every extreme that they name: `send_map`: entries q * 2 to q * 2 + 1 of row (sx, sy, iz) hold, in their first slots, the brick-local voxels (i * 8 + j) * 128 + k of the positions that this brick sends to owner q = ix * 16 + iy of the same iz, and -1 in the others; no voxel appears twice in a row; some brick fills all 2 slots of some owner. `owner_slots`: the 128 entries of owner d = (ix * 16 + iy) * 4 + iz name, each once, exactly the slots src * 2 + slot that the bricks src = sx * 16 + sy with the same iz fill for it.
All inputs are finite; a program needn't handle non-finite values.
Results may differ from a plain program's by a relative error of at most 0.00012.
Values sent between devices are 32-bit elements; how exact they have to be, the bound alone decides.
A program may use at most 64 MiB of HBM per device.

v0:
```python
import jax
import jax.numpy as jnp
from jax import lax
from jax.sharding import Mesh
from jax.sharding import PartitionSpec as P

GX_GY_GZ = ("gx_0", "gx_1", "gy", "gz")
GX = ("gx_0", "gx_1")
GX_GY = ("gx_0", "gx_1", "gy")
mass_term = 0.25


def extended(block, sides, width):
    for axis, dim in sides:
        count = lax.axis_size(axis)
        forward = [(i, i + 1) for i in range(count - 1)]
        backward = [(target, source) for source, target in forward]
        low = lax.ppermute(
            lax.slice_in_dim(block, block.shape[dim] - width, None, axis=dim), axis, forward
        )
        high = lax.ppermute(lax.slice_in_dim(block, 0, width, axis=dim), axis, backward)
        block = jnp.concatenate([low, block, high], axis=dim)
    return block


def by_axis(x, axes):
    for axis in axes:
        x = lax.psum(x, axis)
    return x


def tissue(shifted, table):
    conductivity = jnp.zeros(shifted.shape, table.dtype)
    for tissue_level in range(table.shape[0]):
        conductivity = conductivity + jnp.where(
            shifted == tissue_level + 1, table[tissue_level], 0.0
        )
    inside = (shifted > 0).astype(table.dtype)
    return (conductivity, inside)


def neighbour_slices(dim_index, offset):
    selection = [slice(1, -1), slice(1, -1), slice(1, -1)]
    selection[dim_index] = slice(2, None) if offset > 0 else slice(0, -2)
    return tuple(selection)


def stencil(padded, conductivity, inside):
    leading = (slice(None),) * (padded.ndim - 3)
    middle = (slice(1, -1), slice(1, -1), slice(1, -1))
    centre = padded[leading + middle]
    own_cond = conductivity[middle]
    own_in = inside[middle]
    accumulated = mass_term * centre
    for dim_index in range(3):
        for offset in (-1, 1):
            beside_all = neighbour_slices(dim_index, offset)
            weight = 0.5 * (own_cond + conductivity[beside_all]) * own_in * inside[beside_all]
            accumulated = accumulated + weight * (centre - padded[leading + beside_all])
    return accumulated


def gram_rows(leadfield):
    entry_pairs = ((0, 0), (1, 1), (2, 2), (0, 1), (0, 2), (1, 2))
    return jnp.stack(
        [jnp.sum(leadfield[first] * leadfield[second], axis=0) for first, second in entry_pairs]
    )


def local_inner(first, second):
    return jnp.sum(first * second, axis=(1, 2, 3))


def per_sensor(values):
    return values[:, None, None, None]


def per_device(source_term, labels, conductivity_table, send_map, owner_slots, sensor_data):
    sensors, size_x, size_y, size_z = source_term.shape
    shifted = labels + 1
    label_pad = extended(shifted, ((GX, 0), ("gy", 1), ("gz", 2)), 2)
    conductivity, inside = tissue(label_pad, conductivity_table)
    source_pad = extended(source_term, ((GX, 1), ("gy", 2), ("gz", 3)), 2)
    applied = stencil(source_pad, conductivity, inside)
    inner_cond = conductivity[1:-1, 1:-1, 1:-1]
    inner_in = inside[1:-1, 1:-1, 1:-1]
    twice_applied = stencil(applied, inner_cond, inner_in)
    applied_core = applied[:, 1:-1, 1:-1, 1:-1]
    moment_zero, moment_one, moment_two, moment_three = (
        by_axis(local_inner(source_term, source_term), GX_GY_GZ),
        by_axis(local_inner(source_term, applied_core), GX_GY_GZ),
        by_axis(local_inner(applied_core, applied_core), GX_GY_GZ),
        by_axis(local_inner(applied_core, twice_applied), GX_GY_GZ),
    )
    first_step = moment_zero / moment_one
    residue = first_step * first_step * moment_two - moment_zero
    growth = 1.0 + residue / moment_zero
    curvature = (
        growth * growth * moment_one
        - 2.0 * growth * first_step * moment_two
        + first_step * first_step * moment_three
    )
    second_step = residue / curvature
    source_coef = first_step + second_step * growth
    applied_coef = second_step * first_step
    solution_pad = (
        per_sensor(source_coef) * source_pad[:, 1:-1, 1:-1, 1:-1]
        - per_sensor(applied_coef) * applied
    )
    cond_inner = conductivity[2:-2, 2:-2, 2:-2]
    voxel_local = jnp.maximum(send_map.reshape(-1), 0)
    index_x = voxel_local // (size_y * size_z)
    index_y = voxel_local // size_z % size_y
    index_z = voxel_local % size_z
    stride_y = size_z + 2
    stride_x = (size_y + 2) * (size_z + 2)
    centre = (index_x + 1) * stride_x + (index_y + 1) * stride_y + (index_z + 1)
    flattened = solution_pad.reshape(sensors, -1)
    cond_here = jnp.take(cond_inner.reshape(-1), voxel_local)

    def gradient(stride):
        upper = jnp.take(flattened, centre + stride, axis=1)
        lower = jnp.take(flattened, centre - stride, axis=1)
        return cond_here * ((upper - lower) * 0.5)

    columns = jnp.stack([gradient(stride_x), gradient(stride_y), gradient(1)])
    received = lax.all_to_all(columns, GX_GY, split_axis=2, concat_axis=2, tiled=True)
    owned = jnp.take(received, owner_slots, axis=2)
    projections = jnp.einsum("csp,st->ctp", owned, sensor_data, precision=lax.Precision.HIGHEST)
    return (projections, gram_rows(owned))


def solution(mesh):
    split = Mesh(
        mesh.devices.reshape(4, 2, mesh.shape["gy"], mesh.shape["gz"]), ("gx_0", "gx_1", "gy", "gz")
    )
    in_specs = (
        P(None, GX, "gy", "gz"),
        P(GX, "gy", "gz"),
        P(),
        P(GX, "gy", "gz", None),
        P(GX_GY_GZ),
        P(),
    )
    out_specs = (P(None, None, GX_GY_GZ), P(None, GX_GY_GZ))
    return jax.shard_map(
        per_device, mesh=split, in_specs=in_specs, out_specs=out_specs, check_vma=False
    )
```

profile of v0, /device:TPU:1, one launch (start us, length us, event | category | flops | bytes accessed | tf_op | source)
XLA Modules:
  0.0 224.1 jit_solution(13874952597590977932)
XLA Ops:
  1.4 4.6 %collective-permute-start.6 = (s32[2,8,128]{2,1,0:T(8,128)S(1)}, s32[2,8,128]{2,1,0:T(8,128)S(1)}, u32[]{:S(2)}, u32[]{:S(2)}) collective-permute-start(s32[2,8,128]{2,1,0:T(8,128)S(1)} %get-tuple-element.70), channel_id=1, source_target_pairs={{0,64},{64,128},{128,192},{192,256},{256,320},{320,384},{384,448},... | collective-permute-start | bytes 24584 | tf_op jit(solution)/shard_map/ppermute | solution.py:18
  6.0 5.5 %collective-permute-start.7 = (s32[2,8,128]{2,1,0:T(8,128)S(1)}, s32[2,8,128]{2,1,0:T(8,128)S(1)}, u32[]{:S(2)}, u32[]{:S(2)}) collective-permute-start(s32[2,8,128]{2,1,0:T(8,128)S(1)} %get-tuple-element.71), channel_id=1, source_target_pairs={{64,0},{128,64},{192,128},{256,192},{320,256},{384,320},{448,384},... | collective-permute-start | bytes 24584 | tf_op jit(solution)/shard_map/ppermute | solution.py:21
  12.5 1.9 collective-permute-start
  14.4 2.4 %collective-permute-start.1 = (f32[32,2,8,128]{3,2,1,0:T(8,128)S(1)}, f32[32,2,8,128]{3,2,1,0:T(8,128)S(1)}, u32[]{:S(2)}, u32[]{:S(2)}) collective-permute-start(f32[32,2,8,128]{3,2,1,0:T(8,128)S(1)} %get-tuple-element.52), channel_id=1, source_target_pairs={{64,0},{128,64},{192,128},{256,192},{320,256},{384,320},{448,384},... | collective-permute-start | bytes 786440 | tf_op jit(solution)/shard_map/ppermute | solution.py:21
  27.2 2.6 %collective-permute-done.9 = s32[8,2,128]{2,1,0:T(2,128)S(1)} collective-permute-done((s32[8,2,128]{2,1,0:T(2,128)S(1)}, s32[8,2,128]{2,1,0:T(2,128)S(1)}, u32[]{:S(2)}, u32[]{:S(2)}) %collective-permute-start.9) | collective-permute-done | bytes 8224 | tf_op jit(solution)/shard_map/ppermute | solution.py:21
  30.0 3.1 %collective-permute-start.10 = (s32[8,12,2]{2,1,0:T(8,128)S(1)}, s32[8,12,2]{2,1,0:T(8,128)S(1)}, u32[]{:S(2)}, u32[]{:S(2)}) collective-permute-start(s32[8,12,2]{2,1,0:T(8,128)S(1)} %get-tuple-element.66), channel_id=1, source_target_pairs={{0,1},{1,2},{2,3},{4,5},{5,6},{6,7},{8,9},{9,10},{10,11},{12,13},{... | collective-permute-start | bytes 2312 | tf_op jit(solution)/shard_map/ppermute | solution.py:18
  35.6 3.3 %collective-permute-done.11 = s32[8,12,2]{2,1,0:T(8,128)S(1)} collective-permute-done((s32[8,12,2]{2,1,0:T(8,128)S(1)}, s32[8,12,2]{2,1,0:T(8,128)S(1)}, u32[]{:S(2)}, u32[]{:S(2)}) %collective-permute-start.11) | collective-permute-done | bytes 800 | tf_op jit(solution)/shard_map/ppermute | solution.py:21
  39.1 3.9 %select_add_fusion = f32[8,12,132]{2,1,0:T(8,128)S(1)} fusion(f32[]{:T(128)} %bitcast.8, f32[]{:T(128)} %bitcast.7, f32[]{:T(128)} %bitcast.6, f32[]{:T(128)} %bitcast.5, f32[]{:T(128)} %bitcast.4, f32[]{:T(128)} %bitcast.3, s32[8,12,2]{2,1,0:T(8,128)S(1)} %collective-permute-done.11, s32[8,2,128]{2,1,0:T(2,128)S(1)} %collective-permute-done.9, ...), kind=kLoop, calls=%fused_computation.79 | loop fusion | flops 291456 | bytes 101400 | tf_op jit(solution)/shard_map/add | solution.py:35
  44.5 3.6 %collective-permute-start.2 = (f32[32,8,2,128]{3,1,2,0:T(8,128)S(1)}, f32[32,8,2,128]{3,1,2,0:T(8,128)S(1)}, u32[]{:S(2)}, u32[]{:S(2)}) collective-permute-start(f32[32,8,2,128]{3,1,2,0:T(8,128)S(1)} %get-tuple-element.49), channel_id=1, source_target_pairs={{0,4},{4,8},{8,12},{12,16},{16,20},{20,24},{24,28},{28,32},{32,36}... | collective-permute-start | bytes 786440 | tf_op jit(solution)/shard_map/ppermute | solution.py:18
  53.1 5.7 %collective-permute-done.3 = f32[32,8,2,128]{3,1,2,0:T(8,128)S(1)} collective-permute-done((f32[32,8,2,128]{3,1,2,0:T(8,128)S(1)}, f32[32,8,2,128]{3,1,2,0:T(8,128)S(1)}, u32[]{:S(2)}, u32[]{:S(2)}) %collective-permute-start.3) | collective-permute-done | bytes 262176 | tf_op jit(solution)/shard_map/ppermute | solution.py:21
  61.6 2.2 copy.93
  66.0 4.2 %collective-permute-start.4 = (f32[32,8,12,2]{0,1,3,2:T(8,128)S(1)}, f32[32,8,12,2]{0,1,3,2:T(8,128)S(1)}, u32[]{:S(2)}, u32[]{:S(2)}) collective-permute-start(f32[32,8,12,2]{0,1,3,2:T(8,128)S(1)} %copy.93), channel_id=1, source_target_pairs={{0,1},{1,2},{2,3},{4,5},{5,6},{6,7},{8,9},{9,10},{10,11},{12,13},{... | collective-permute-start | bytes 73736 | tf_op jit(solution)/shard_map/ppermute | solution.py:18
  76.6 2.4 %copy.95 = f32[32,8,12,2]{3,1,2,0:T(8,128)} copy(f32[32,8,12,2]{0,1,3,2:T(8,128)S(1)} %collective-permute-done.4) | data formatting | bytes 49152 | tf_op jit(solution)/shard_map/ppermute | solution.py:18
  78.9 2.4 %copy.96 = f32[32,8,12,2]{3,1,2,0:T(8,128)} copy(f32[32,8,12,2]{0,1,3,2:T(8,128)S(1)} %collective-permute-done.5) | data formatting | bytes 49152 | tf_op jit(solution)/shard_map/ppermute | solution.py:21
  81.4 4.8 %pad_maximum_fusion = f32[32,8,12,132]{3,1,2,0:T(8,128)S(1)} fusion(f32[32,8,12,2]{3,1,2,0:T(8,128)} %copy.96, f32[32,8,2,128]{3,1,2,0:T(8,128)} %copy-done.11, f32[32,2,8,128]{3,1,2,0:T(2,128)} %copy-done.7, f32[32,4,8,128]{3,1,2,0:T(4,128)} %copy-done.4, f32[32,2,8,128]{3,1,2,0:T(2,128)S(1)} %copy.90, f32[32,8,2,128]{3,1,2,0:T(8,128)} %copy-done.9, ...), kind=kLoop, calls=%fused_computation.8 | loop fusion | flops 2433024 | bytes 3244032 | tf_op jit(solution)/shard_map/concatenate | solution.py:22
  86.3 7.2 %fusion.2 = f32[32,6,10,130]{3,1,2,0:T(8,128)S(1)} fusion(f32[32,8,12,2]{3,1,2,0:T(8,128)S(1)} %copy-done.3, f32[32,8,2,128]{3,1,2,0:T(8,128)S(1)} %copy-done.12, f32[32,8,2,128]{3,1,2,0:T(8,128)S(1)} %copy-done.10, f32[32,2,8,128]{3,1,2,0:T(2,128)S(1)} %copy-done.8, f32[32,4,8,128]{3,1,2,0:T(4,128)S(1)} %copy-done.5, f32[32,2,8,128]{3,1,2,0:T(2,128)S(1)} %copy.90, ...), kind=kLoop, calls=%fused_computation.12 | loop fusion | flops 7238400 | bytes 7799616 | tf_op jit(solution)/shard_map/add | solution.py:59
  95.1 2.4 %multiply_reduce_fusion.1 = (f32[32]{0:T(128)S(1)}, f32[32]{0:T(128)S(1)}, f32[32]{0:T(128)S(1)}) fusion(f32[32,6,10,130]{3,1,2,0:T(8,128)S(1)} %fusion.2, f32[32,4,8,128]{3,2,1,0:T(8,128)S(1)} %copy-done.6, f32[4,8,128]{2,0,1:T(4,128)S(1)} %copy.111, f32[4,8,128]{2,0,1:T(4,128)S(1)} %copy.110, f32[4,8,128]{2,0,1:T(4,128)S(1)} %copy-done.19, ...), kind=kLoop, calls=%fused_computation.60 | loop fusion | flops 3276704 | bytes 4292992 | tf_op jit(solution)/shard_map/reduce_sum | solution.py:71
  97.5 6.0 %all-reduce.2 = (f32[32]{0:T(128)S(1)}, f32[32]{0:T(128)S(1)}, f32[32]{0:T(128)S(1)}, f32[32]{0:T(128)S(1)}) all-reduce(f32[32]{0:T(128)S(1)} %get-tuple-element.15, f32[32]{0:T(128)S(1)} %get-tuple-element.14, f32[32]{0:T(128)S(1)} %copy-done.32, ...), channel_id=1, replica_groups=mesh['gx_0'=4,'gx_1'=2,'gy'=16,'gz'=4] {'gx_0'}, use_global_device_ids=true, to_apply=%region_16.17 | all-reduce | flops 128 | bytes 1024 | tf_op jit(solution)/shard_map/psum | solution.py:28
  103.5 8.6 %all-reduce.3 = (f32[32]{0:T(128)S(1)}, f32[32]{0:T(128)S(1)}, f32[32]{0:T(128)S(1)}, f32[32]{0:T(128)S(1)}) all-reduce(f32[32]{0:T(128)S(1)} %get-tuple-element.33, f32[32]{0:T(128)S(1)} %get-tuple-element.34, f32[32]{0:T(128)S(1)} %get-tuple-element.35, ...), channel_id=1, replica_groups=mesh['gx_0'=4,'gx_1'=2,'gy'=16,'gz'=4] {'gx_1'}, use_global_device_ids=true, to_apply=%region_17.18 | all-reduce | flops 128 | bytes 1024 | tf_op jit(solution)/shard_map/psum | solution.py:28
  112.0 26.8 %all-reduce = (f32[32]{0:T(128)S(1)}, f32[32]{0:T(128)S(1)}, f32[32]{0:T(128)S(1)}, f32[32]{0:T(128)S(1)}) all-reduce(f32[32]{0:T(128)S(1)} %get-tuple-element.37, f32[32]{0:T(128)S(1)} %get-tuple-element.38, f32[32]{0:T(128)S(1)} %get-tuple-element.39, ...), channel_id=1, replica_groups=mesh['gx_0'=4,'gx_1'=2,'gy'=16,'gz'=4] {'gy'}, use_global_device_ids=true, to_apply=%region_18.19 | all-reduce | flops 128 | bytes 1024 | tf_op jit(solution)/shard_map/psum | solution.py:28
  138.9 7.4 %all-reduce.1 = (f32[32]{0:T(128)S(1)}, f32[32]{0:T(128)S(1)}, f32[32]{0:T(128)S(1)}, f32[32]{0:T(128)S(1)}) all-reduce(f32[32]{0:T(128)S(1)} %get-tuple-element.25, f32[32]{0:T(128)S(1)} %get-tuple-element.26, f32[32]{0:T(128)S(1)} %get-tuple-element.27, ...), channel_id=1, replica_groups=mesh['gx_0'=4,'gx_1'=2,'gy'=16,'gz'=4] {'gz'}, use_global_device_ids=true, to_apply=%region_19.20 | all-reduce | flops 128 | bytes 1024 | tf_op jit(solution)/shard_map/psum | solution.py:28
  146.3 4.1 %multiply_subtract_fusion = f32[32,6,10,130]{3,1,2,0:T(8,128)} fusion(f32[32,6,10,130]{3,1,2,0:T(8,128)} %copy-done.1, f32[32,8,12,132]{3,1,2,0:T(8,128)S(1)} %pad_maximum_fusion, f32[32]{0:T(128)S(1)} %mul.415, f32[32]{0:T(128)S(1)} %get-tuple-element.43), kind=kLoop, calls=%fused_computation.37 | loop fusion | flops 748800 | bytes 2995456 | tf_op jit(solution)/shard_map/sub | solution.py:107
  150.5 4.8 %copy.122 = f32[32,6,10,130]{0,3,2,1:T(8,128)} copy(f32[32,6,10,130]{3,1,2,0:T(8,128)} %multiply_subtract_fusion) | data formatting | bytes 1996800 | tf_op jit(solution)/shard_map/reshape | solution.py:118
  155.3 4.8 %reshape.172 = f32[32,7800]{0,1:T(8,128)} reshape(f32[32,6,10,130]{0,3,2,1:T(8,128)} %copy.122) | data formatting | bytes 1996800 | tf_op jit(solution)/shard_map/reshape | solution.py:118
  160.1 3.0 %gather_fusion.7 = f32[256,32]{1,0:T(8,128)S(1)} fusion(f32[32,7800]{0,1:T(8,128)} %reshape.172, s32[1024]{0:T(1024)} %get-tuple-element.96), kind=kCustom, calls=%fused_computation.5.clone | custom fusion | bytes 66560 | tf_op jit(solution)/shard_map/jit(_take)/gather | solution.py:123
  163.0 3.0 %gather_fusion.6 = f32[256,32]{1,0:T(8,128)S(1)} fusion(f32[32,7800]{0,1:T(8,128)} %reshape.172, s32[1024]{0:T(1024)} %get-tuple-element.97), kind=kCustom, calls=%fused_computation.4.clone | custom fusion | bytes 66560 | tf_op jit(solution)/shard_map/jit(_take)/gather | solution.py:122
  166.0 3.0 %gather_fusion.5 = f32[256,32]{1,0:T(8,128)S(1)} fusion(f32[32,7800]{0,1:T(8,128)} %reshape.172, s32[1024]{0:T(1024)} %get-tuple-element.98), kind=kCustom, calls=%fused_computation.3.clone | custom fusion | bytes 66560 | tf_op jit(solution)/shard_map/jit(_take)/gather | solution.py:123
  169.0 3.0 %gather_fusion.4 = f32[256,32]{1,0:T(8,128)S(1)} fusion(f32[32,7800]{0,1:T(8,128)} %reshape.172, s32[1024]{0:T(1024)} %get-tuple-element.99), kind=kCustom, calls=%fused_computation.2.clone | custom fusion | bytes 66560 | tf_op jit(solution)/shard_map/jit(_take)/gather | solution.py:122
  172.0 3.0 %gather_fusion.3 = f32[256,32]{1,0:T(8,128)S(1)} fusion(f32[32,7800]{0,1:T(8,128)} %reshape.172, s32[1024]{0:T(1024)} %get-tuple-element.100), kind=kCustom, calls=%fused_computation.1.clone | custom fusion | bytes 66560 | tf_op jit(solution)/shard_map/jit(_take)/gather | solution.py:123
  175.0 3.0 %gather_fusion.2 = f32[256,32]{1,0:T(8,128)S(1)} fusion(f32[32,7800]{0,1:T(8,128)} %reshape.172, s32[1024]{0:T(1024)} %get-tuple-element.101), kind=kCustom, calls=%fused_computation.clone | custom fusion | bytes 66560 | tf_op jit(solution)/shard_map/jit(_take)/gather | solution.py:122
  179.8 20.1 %all-to-all-start = ((f32[128,1,192]{2,1,0:T(1,128)}), f32[128,1,192]{2,1,0:T(1,128)S(1)}, u32[]{:S(2)}, u32[]{:S(2)}) async-start(f32[128,1,192]{2,1,0:T(1,128)} %reshape.176), calls=%async_computation | async-start | bytes 262144 | tf_op jit(solution)/shard_map/all_to_all | solution.py:127
  199.9 18.2 %all-to-all-done = f32[128,1,192]{2,1,0:T(1,128)S(1)} async-done(((f32[128,1,192]{2,1,0:T(1,128)}), f32[128,1,192]{2,1,0:T(1,128)S(1)}, u32[]{:S(2)}, u32[]{:S(2)}) %all-to-all-start) | async-done | bytes 98336 | tf_op jit(solution)/shard_map/all_to_all | solution.py:127
  (146 shorter events, 42.0 us)
Async XLA Ops:
  0.6 221.8 %copy-start = (f32[32,128]{1,0:T(8,128)S(1)}, f32[32,128]{1,0:T(8,128)}, u32[]{:S(2)}) copy-start(f32[32,128]{1,0:T(8,128)} %param.13) | copy-start | bytes 49156
  1.4 22.6 %collective-permute-start.6 = (s32[2,8,128]{2,1,0:T(8,128)S(1)}, s32[2,8,128]{2,1,0:T(8,128)S(1)}, u32[]{:S(2)}, u32[]{:S(2)}) collective-permute-start(s32[2,8,128]{2,1,0:T(8,128)S(1)} %get-tuple-element.70), channel_id=1, source_target_pairs={{0,64},{64,128},{128,192},{192,256},{256,320},{320,384},{384,448},... | collective-permute-start | bytes 24584 | tf_op jit(solution)/shard_map/ppermute | solution.py:18
  6.0 18.1 %collective-permute-start.7 = (s32[2,8,128]{2,1,0:T(8,128)S(1)}, s32[2,8,128]{2,1,0:T(8,128)S(1)}, u32[]{:S(2)}, u32[]{:S(2)}) collective-permute-start(s32[2,8,128]{2,1,0:T(8,128)S(1)} %get-tuple-element.71), channel_id=1, source_target_pairs={{64,0},{128,64},{192,128},{256,192},{320,256},{384,320},{448,384},... | collective-permute-start | bytes 24584 | tf_op jit(solution)/shard_map/ppermute | solution.py:21
  12.5 31.5 %collective-permute-start = (f32[32,2,8,128]{3,2,1,0:T(8,128)S(1)}, f32[32,2,8,128]{3,2,1,0:T(8,128)S(1)}, u32[]{:S(2)}, u32[]{:S(2)}) collective-permute-start(f32[32,2,8,128]{3,2,1,0:T(8,128)S(1)} %get-tuple-element.51), channel_id=1, source_target_pairs={{0,64},{64,128},{128,192},{192,256},{256,320},{320,384},{384,448},... | collective-permute-start | bytes 786440 | tf_op jit(solution)/shard_map/ppermute | solution.py:18
  14.4 29.7 %collective-permute-start.1 = (f32[32,2,8,128]{3,2,1,0:T(8,128)S(1)}, f32[32,2,8,128]{3,2,1,0:T(8,128)S(1)}, u32[]{:S(2)}, u32[]{:S(2)}) collective-permute-start(f32[32,2,8,128]{3,2,1,0:T(8,128)S(1)} %get-tuple-element.52), channel_id=1, source_target_pairs={{64,0},{128,64},{192,128},{256,192},{320,256},{384,320},{448,384},... | collective-permute-start | bytes 786440 | tf_op jit(solution)/shard_map/ppermute | solution.py:21
  24.0 3.2 %collective-permute-start.8 = (s32[8,2,128]{2,1,0:T(2,128)S(1)}, s32[8,2,128]{2,1,0:T(2,128)S(1)}, u32[]{:S(2)}, u32[]{:S(2)}) collective-permute-start(s32[8,2,128]{2,1,0:T(2,128)S(1)} %get-tuple-element.68), channel_id=1, source_target_pairs={{0,4},{4,8},{8,12},{12,16},{16,20},{20,24},{24,28},{28,32},{32,36}... | collective-permute-start | bytes 24584 | tf_op jit(solution)/shard_map/ppermute | solution.py:18
  25.3 4.5 %collective-permute-start.9 = (s32[8,2,128]{2,1,0:T(2,128)S(1)}, s32[8,2,128]{2,1,0:T(2,128)S(1)}, u32[]{:S(2)}, u32[]{:S(2)}) collective-permute-start(s32[8,2,128]{2,1,0:T(2,128)S(1)} %get-tuple-element.69), channel_id=1, source_target_pairs={{4,0},{8,4},{12,8},{16,12},{20,16},{24,20},{28,24},{32,28},{36,32}... | collective-permute-start | bytes 24584 | tf_op jit(solution)/shard_map/ppermute | solution.py:21
  30.0 5.6 %collective-permute-start.10 = (s32[8,12,2]{2,1,0:T(8,128)S(1)}, s32[8,12,2]{2,1,0:T(8,128)S(1)}, u32[]{:S(2)}, u32[]{:S(2)}) collective-permute-start(s32[8,12,2]{2,1,0:T(8,128)S(1)} %get-tuple-element.66), channel_id=1, source_target_pairs={{0,1},{1,2},{2,3},{4,5},{5,6},{6,7},{8,9},{9,10},{10,11},{12,13},{... | collective-permute-start | bytes 2312 | tf_op jit(solution)/shard_map/ppermute | solution.py:18
  33.1 5.9 %collective-permute-start.11 = (s32[8,12,2]{2,1,0:T(8,128)S(1)}, s32[8,12,2]{2,1,0:T(8,128)S(1)}, u32[]{:S(2)}, u32[]{:S(2)}) collective-permute-start(s32[8,12,2]{2,1,0:T(8,128)S(1)} %get-tuple-element.67), channel_id=1, source_target_pairs={{1,0},{2,1},{3,2},{5,4},{6,5},{7,6},{9,8},{10,9},{11,10},{13,12},{... | collective-permute-start | bytes 2312 | tf_op jit(solution)/shard_map/ppermute | solution.py:21
  35.6 23.3 %copy-start.4 = (f32[32,4,8,128]{3,1,2,0:T(4,128)}, f32[32,4,8,128]{3,1,2,0:T(4,128)S(1)}, u32[]{:S(2)}) copy-start(f32[32,4,8,128]{3,1,2,0:T(4,128)S(1)} %copy.105) | copy-start | bytes 1572868
  44.3 15.6 %copy-start.7 = (f32[32,2,8,128]{3,1,2,0:T(2,128)}, f32[32,2,8,128]{3,1,2,0:T(2,128)S(1)}, u32[]{:S(2)}) copy-start(f32[32,2,8,128]{3,1,2,0:T(2,128)S(1)} %copy.92) | copy-start | bytes 786436
  44.5 8.6 %collective-permute-start.2 = (f32[32,8,2,128]{3,1,2,0:T(8,128)S(1)}, f32[32,8,2,128]{3,1,2,0:T(8,128)S(1)}, u32[]{:S(2)}, u32[]{:S(2)}) collective-permute-start(f32[32,8,2,128]{3,1,2,0:T(8,128)S(1)} %get-tuple-element.49), channel_id=1, source_target_pairs={{0,4},{4,8},{8,12},{12,16},{16,20},{20,24},{24,28},{28,32},{32,36}... | collective-permute-start | bytes 786440 | tf_op jit(solution)/shard_map/ppermute | solution.py:18
  48.0 10.8 %collective-permute-start.3 = (f32[32,8,2,128]{3,1,2,0:T(8,128)S(1)}, f32[32,8,2,128]{3,1,2,0:T(8,128)S(1)}, u32[]{:S(2)}, u32[]{:S(2)}) collective-permute-start(f32[32,8,2,128]{3,1,2,0:T(8,128)S(1)} %get-tuple-element.50), channel_id=1, source_target_pairs={{4,0},{8,4},{12,8},{16,12},{20,16},{24,20},{28,24},{32,28},{36,32}... | collective-permute-start | bytes 786440 | tf_op jit(solution)/shard_map/ppermute | solution.py:21
  61.6 9.1 %copy-start.25 = (f32[4,8,128]{2,1,0:T(8,128)S(1)}, f32[4,8,128]{2,1,0:T(8,128)}, u32[]{:S(2)}) copy-start(f32[4,8,128]{2,1,0:T(8,128)} %get-tuple-element.58) | copy-start | bytes 49156
  61.6 9.1 %copy-start.24 = (f32[4,8,128]{2,1,0:T(8,128)S(1)}, f32[4,8,128]{2,1,0:T(8,128)}, u32[]{:S(2)}) copy-start(f32[4,8,128]{2,1,0:T(8,128)} %get-tuple-element.53) | copy-start | bytes 49156
  61.6 9.7 %copy-start.23 = (f32[4,8,128]{2,1,0:T(8,128)S(1)}, f32[4,8,128]{2,1,0:T(8,128)}, u32[]{:S(2)}) copy-start(f32[4,8,128]{2,1,0:T(8,128)} %get-tuple-element.54) | copy-start | bytes 49156
  61.6 10.3 %copy-start.22 = (f32[4,8,128]{2,1,0:T(8,128)S(1)}, f32[4,8,128]{2,1,0:T(8,128)}, u32[]{:S(2)}) copy-start(f32[4,8,128]{2,1,0:T(8,128)} %get-tuple-element.55) | copy-start | bytes 49156
  64.7 14.2 %collective-permute-start.5 = (f32[32,8,12,2]{0,1,3,2:T(8,128)S(1)}, f32[32,8,12,2]{0,1,3,2:T(8,128)S(1)}, u32[]{:S(2)}, u32[]{:S(2)}) collective-permute-start(f32[32,8,12,2]{0,1,3,2:T(8,128)S(1)} %copy.94), channel_id=1, source_target_pairs={{1,0},{2,1},{3,2},{5,4},{6,5},{7,6},{9,8},{10,9},{11,10},{13,12},{... | collective-permute-start | bytes 73736 | tf_op jit(solution)/shard_map/ppermute | solution.py:21
  66.0 10.5 %collective-permute-start.4 = (f32[32,8,12,2]{0,1,3,2:T(8,128)S(1)}, f32[32,8,12,2]{0,1,3,2:T(8,128)S(1)}, u32[]{:S(2)}, u32[]{:S(2)}) collective-permute-start(f32[32,8,12,2]{0,1,3,2:T(8,128)S(1)} %copy.93), channel_id=1, source_target_pairs={{0,1},{1,2},{2,3},{4,5},{5,6},{6,7},{8,9},{9,10},{10,11},{12,13},{... | collective-permute-start | bytes 73736 | tf_op jit(solution)/shard_map/ppermute | solution.py:18
  86.3 8.8 %copy-start.6 = (f32[32,4,8,128]{3,2,1,0:T(8,128)S(1)}, f32[32,4,8,128]{3,2,1,0:T(8,128)}, u32[]{:S(2)}) copy-start(f32[32,4,8,128]{3,2,1,0:T(8,128)} %param.8) | copy-start | bytes 1572868
  86.3 8.8 %copy-start.18 = (f32[4,8,128]{2,0,1:T(4,128)S(1)}, f32[4,8,128]{2,0,1:T(4,128)}, u32[]{:S(2)}) copy-start(f32[4,8,128]{2,0,1:T(4,128)} %copy.106) | copy-start | bytes 49156
  86.3 8.8 %copy-start.19 = (f32[4,8,128]{2,0,1:T(4,128)S(1)}, f32[4,8,128]{2,0,1:T(4,128)}, u32[]{:S(2)}) copy-start(f32[4,8,128]{2,0,1:T(4,128)} %copy.109) | copy-start | bytes 49156
  86.3 8.8 %copy-start.20 = (f32[4,8,128]{2,0,1:T(4,128)S(1)}, f32[4,8,128]{2,0,1:T(4,128)}, u32[]{:S(2)}) copy-start(f32[4,8,128]{2,0,1:T(4,128)} %copy.108) | copy-start | bytes 49156
  155.2 22.8 %copy-start.26 = (f32[256]{0:T(256)S(1)}, f32[256]{0:T(256)}, u32[]{:S(2)}) copy-start(f32[256]{0:T(256)} %select_multiply_fusion) | copy-start | bytes 3076
  155.2 22.8 %copy-start.27 = (pred[256]{0:T(512)(128)(4,1)S(1)}, pred[256]{0:T(512)(128)(4,1)}, u32[]{:S(2)}) copy-start(pred[256]{0:T(512)(128)(4,1)} %get-tuple-element.75) | copy-start | bytes 772
  155.2 22.8 %copy-start.28 = (pred[256]{0:T(512)(128)(4,1)S(1)}, pred[256]{0:T(512)(128)(4,1)}, u32[]{:S(2)}) copy-start(pred[256]{0:T(512)(128)(4,1)} %get-tuple-element.76) | copy-start | bytes 772
  155.2 22.8 %copy-start.29 = (pred[256]{0:T(512)(128)(4,1)S(1)}, pred[256]{0:T(512)(128)(4,1)}, u32[]{:S(2)}) copy-start(pred[256]{0:T(512)(128)(4,1)} %get-tuple-element.77) | copy-start | bytes 772
  155.3 22.8 %copy-start.30 = (pred[256]{0:T(512)(128)(4,1)S(1)}, pred[256]{0:T(512)(128)(4,1)}, u32[]{:S(2)}) copy-start(pred[256]{0:T(512)(128)(4,1)} %get-tuple-element.78) | copy-start | bytes 772
  155.3 22.8 %copy-start.31 = (pred[256]{0:T(512)(128)(4,1)S(1)}, pred[256]{0:T(512)(128)(4,1)}, u32[]{:S(2)}) copy-start(pred[256]{0:T(512)(128)(4,1)} %get-tuple-element.79) | copy-start | bytes 772
  155.3 22.8 %copy-start.33 = (pred[256]{0:T(512)(128)(4,1)S(1)}, pred[256]{0:T(512)(128)(4,1)}, u32[]{:S(2)}) copy-start(pred[256]{0:T(512)(128)(4,1)} %get-tuple-element.41) | copy-start | bytes 772
  163.0 36.8 %copy-start.34 = (s32[128]{0:T(128)S(1)}, s32[128]{0:T(128)}, u32[]{:S(2)}) copy-start(s32[128]{0:T(128)} %param.12) | copy-start | bytes 1540
  179.8 38.3 %all-to-all-start = ((f32[128,1,192]{2,1,0:T(1,128)}), f32[128,1,192]{2,1,0:T(1,128)S(1)}, u32[]{:S(2)}, u32[]{:S(2)}) async-start(f32[128,1,192]{2,1,0:T(1,128)} %reshape.176), calls=%async_computation | async-start | bytes 262144 | tf_op jit(solution)/shard_map/all_to_all | solution.py:127
  (16 other events, 73.0 us)
where the time goes:
time: 225 us; the launch traced here: 224 us
  local copies, waits for them, and re-layouts  55.3 us (25%)
  starting transfers between devices  51.7 us (23%)
  blocking collectives  48.8 us (22%)
  other arithmetic  35.7 us (16%)
  waiting for transfers between devices  31 us (14%)
    psum x4, blocking collectives, by_axis(): x = lax.psum(x, axis)  48.8 us
    all_to_all x1, starting transfers between devices, per_device(): lax.all_to_all(columns, GX_GY, split_axis=2, concat_axis=2, tiled=True)  20.1 us
    ppermute x6, starting transfers between devices, extended(): lax.ppermute(lax.slice_in_dim(block, block.shape[dim] - width, None, axis...  18.6 us
    all_to_all x1, waiting for transfers between devices, per_device(): lax.all_to_all(columns, GX_GY, split_axis=2, concat_axis=2, tiled=True)  18.2 us
    ppermute x6, starting transfers between devices, extended(): lax.ppermute(lax.slice_in_dim(block, 0, width, axis=dim), axis, backward)  13 us
    ppermute x6, waiting for transfers between devices, extended(): lax.ppermute(lax.slice_in_dim(block, 0, width, axis=dim), axis, backward)  11.7 us
    reshape x2, local copies, waits for them, and re-layouts, per_device(): flattened = solution_pad.reshape(sensors, -1)  9.55 us
    gather x3, local copies, waits for them, and re-layouts, gradient(): upper = jnp.take(flattened, centre + stride, axis=1)  8.98 us
  transfers between devices with their start and end apart: 13, of which 5 were waited for; matrix products, arithmetic and copies ran while one was open for 12% of the time, Pallas kernels for 0%

commit v1 on v0

--- a/solution.py
+++ b/solution.py
@@ -25,7 +25,8 @@
 
 def by_axis(x, axes):
     for axis in axes:
-        x = lax.psum(x, axis)
+        shards = lax.all_gather(x, axis)
+        x = jnp.sum(shards, axis=0)
     return x
 
 

time: 225 us -> 236 us (1.049)
  local copies, waits for them, and re-layouts: 55.3 us -> 66 us
  waiting for transfers between devices: 31 us -> 26.5 us
  between operations: 1.36 us -> 3.91 us
    unnamed x0 -> x4, blocking collectives: none -> 50.4 us
    psum x4 -> x0, blocking collectives: 48.8 us -> none  [by_axis(): x = lax.psum(x, axis)]
    unnamed x74 -> x112, local copies, waits for them, and re-layouts: 5.64 us -> 15 us
    ppermute x6, waiting for transfers between devices: 11.7 us -> 6.34 us  [extended(): lax.ppermute(lax.slice_in_dim(block, 0, width, axis=dim), axis, backward)]
  transfers between devices with their start and end apart: 13 -> 13, of which waited for: 5 -> 4; matrix products, arithmetic and copies ran while one was open for 12% -> 14% of each run, Pallas kernels for 0% -> 0%
where the time goes in v1:
time: 236 us; the launch traced here: 234 us
  local copies, waits for them, and re-layouts  66 us (28%)
  starting transfers between devices  51.6 us (22%)
  blocking collectives  50.4 us (21%)
  other arithmetic  35.6 us (15%)
  waiting for transfers between devices  26.5 us (11%)
  between operations  3.91 us (2%)
    unnamed x4, blocking collectives  50.4 us
    all_to_all x1, starting transfers between devices, per_device(): lax.all_to_all(columns, GX_GY, split_axis=2, concat_axis=2, tiled=True)  19.6 us
    ppermute x6, starting transfers between devices, extended(): lax.ppermute(lax.slice_in_dim(block, block.shape[dim] - width, None, axis...  19 us
    all_to_all x1, waiting for transfers between devices, per_device(): lax.all_to_all(columns, GX_GY, split_axis=2, concat_axis=2, tiled=True)  18.2 us
    unnamed x112, local copies, waits for them, and re-layouts  15 us
    ppermute x6, starting transfers between devices, extended(): lax.ppermute(lax.slice_in_dim(block, 0, width, axis=dim), axis, backward)  13 us
    reshape x2, local copies, waits for them, and re-layouts, per_device(): flattened = solution_pad.reshape(sensors, -1)  9.57 us
    gather x3, local copies, waits for them, and re-layouts, gradient(): upper = jnp.take(flattened, centre + stride, axis=1)  8.98 us
  transfers between devices with their start and end apart: 13, of which 4 were waited for; matrix products, arithmetic and copies ran while one was open for 14% of the time, Pallas kernels for 0%

profile of v1, /device:TPU:1, one launch (start us, length us, event | category | flops | bytes accessed | tf_op | source)
XLA Modules:
  0.0 234.2 jit_solution(8973652074910323684)
XLA Ops:
  1.4 4.6 %collective-permute-start.6 = (s32[2,8,128]{2,1,0:T(8,128)S(1)}, s32[2,8,128]{2,1,0:T(8,128)S(1)}, u32[]{:S(2)}, u32[]{:S(2)}) collective-permute-start(s32[2,8,128]{2,1,0:T(8,128)S(1)} %get-tuple-element.70), channel_id=1, source_target_pairs={{0,64},{64,128},{128,192},{192,256},{256,320},{320,384},{384,448},... | collective-permute-start | bytes 24584 | tf_op jit(solution)/shard_map/ppermute | solution.py:18
  6.0 5.5 %collective-permute-start.7 = (s32[2,8,128]{2,1,0:T(8,128)S(1)}, s32[2,8,128]{2,1,0:T(8,128)S(1)}, u32[]{:S(2)}, u32[]{:S(2)}) collective-permute-start(s32[2,8,128]{2,1,0:T(8,128)S(1)} %get-tuple-element.71), channel_id=1, source_target_pairs={{64,0},{128,64},{192,128},{256,192},{320,256},{384,320},{448,384},... | collective-permute-start | bytes 24584 | tf_op jit(solution)/shard_map/ppermute | solution.py:21
  12.5 1.9 collective-permute-start
  14.4 2.4 %collective-permute-start.1 = (f32[32,2,8,128]{3,2,1,0:T(8,128)S(1)}, f32[32,2,8,128]{3,2,1,0:T(8,128)S(1)}, u32[]{:S(2)}, u32[]{:S(2)}) collective-permute-start(f32[32,2,8,128]{3,2,1,0:T(8,128)S(1)} %get-tuple-element.52), channel_id=1, source_target_pairs={{64,0},{128,64},{192,128},{256,192},{320,256},{384,320},{448,384},... | collective-permute-start | bytes 786440 | tf_op jit(solution)/shard_map/ppermute | solution.py:21
  30.1 3.1 %collective-permute-start.10 = (s32[8,12,2]{2,1,0:T(8,128)S(1)}, s32[8,12,2]{2,1,0:T(8,128)S(1)}, u32[]{:S(2)}, u32[]{:S(2)}) collective-permute-start(s32[8,12,2]{2,1,0:T(8,128)S(1)} %get-tuple-element.66), channel_id=1, source_target_pairs={{0,1},{1,2},{2,3},{4,5},{5,6},{6,7},{8,9},{9,10},{10,11},{12,13},{... | collective-permute-start | bytes 2312 | tf_op jit(solution)/shard_map/ppermute | solution.py:18
  41.8 3.9 %select_add_fusion = f32[8,12,132]{2,1,0:T(8,128)S(1)} fusion(f32[]{:T(128)} %bitcast.12, f32[]{:T(128)} %bitcast.11, f32[]{:T(128)} %bitcast.10, f32[]{:T(128)} %bitcast.9, f32[]{:T(128)} %bitcast.8, f32[]{:T(128)} %bitcast.7, s32[8,12,2]{2,1,0:T(8,128)S(1)} %collective-permute-done.11, s32[8,2,128]{2,1,0:T(2,128)S(1)} %collective-permute-done.9, ...), kind=kLoop, calls=%fused_computation.79 | loop fusion | flops 291456 | bytes 101400 | tf_op jit(solution)/shard_map/add | solution.py:36
  47.1 3.6 %collective-permute-start.2 = (f32[32,8,2,128]{3,1,2,0:T(8,128)S(1)}, f32[32,8,2,128]{3,1,2,0:T(8,128)S(1)}, u32[]{:S(2)}, u32[]{:S(2)}) collective-permute-start(f32[32,8,2,128]{3,1,2,0:T(8,128)S(1)} %get-tuple-element.49), channel_id=1, source_target_pairs={{0,4},{4,8},{8,12},{12,16},{16,20},{20,24},{24,28},{28,32},{32,36}... | collective-permute-start | bytes 786440 | tf_op jit(solution)/shard_map/ppermute | solution.py:18
  52.7 1.7 gather_fusion
  54.7 1.9 collective-permute-done.2
  56.6 5.6 %collective-permute-done.3 = f32[32,8,2,128]{3,1,2,0:T(8,128)S(1)} collective-permute-done((f32[32,8,2,128]{3,1,2,0:T(8,128)S(1)}, f32[32,8,2,128]{3,1,2,0:T(8,128)S(1)}, u32[]{:S(2)}, u32[]{:S(2)}) %collective-permute-start.3) | collective-permute-done | bytes 262176 | tf_op jit(solution)/shard_map/ppermute | solution.py:21
  65.0 2.2 copy.93
  69.4 4.5 %collective-permute-start.4 = (f32[32,8,12,2]{0,1,3,2:T(8,128)S(1)}, f32[32,8,12,2]{0,1,3,2:T(8,128)S(1)}, u32[]{:S(2)}, u32[]{:S(2)}) collective-permute-start(f32[32,8,12,2]{0,1,3,2:T(8,128)S(1)} %copy.93), channel_id=1, source_target_pairs={{0,1},{1,2},{2,3},{4,5},{5,6},{6,7},{8,9},{9,10},{10,11},{12,13},{... | collective-permute-start | bytes 73736 | tf_op jit(solution)/shard_map/ppermute | solution.py:18
  80.4 2.4 %copy.95 = f32[32,8,12,2]{3,1,2,0:T(8,128)} copy(f32[32,8,12,2]{0,1,3,2:T(8,128)S(1)} %collective-permute-done.4) | data formatting | bytes 49152 | tf_op jit(solution)/shard_map/ppermute | solution.py:18
  82.7 2.4 %copy.96 = f32[32,8,12,2]{3,1,2,0:T(8,128)} copy(f32[32,8,12,2]{0,1,3,2:T(8,128)S(1)} %collective-permute-done.5) | data formatting | bytes 49152 | tf_op jit(solution)/shard_map/ppermute | solution.py:21
  85.2 4.8 %pad_maximum_fusion = f32[32,8,12,132]{3,1,2,0:T(8,128)S(1)} fusion(f32[32,8,12,2]{3,1,2,0:T(8,128)} %copy.96, f32[32,8,2,128]{3,1,2,0:T(8,128)} %copy-done.11, f32[32,2,8,128]{3,1,2,0:T(2,128)} %copy-done.7, f32[32,4,8,128]{3,1,2,0:T(4,128)} %copy-done.4, f32[32,2,8,128]{3,1,2,0:T(2,128)S(1)} %copy.90, f32[32,8,2,128]{3,1,2,0:T(8,128)} %copy-done.9, ...), kind=kLoop, calls=%fused_computation.8 | loop fusion | flops 2433024 | bytes 3244032 | tf_op jit(solution)/shard_map/concatenate | solution.py:22
  90.2 7.2 %fusion.2 = f32[32,6,10,130]{3,1,2,0:T(8,128)S(1)} fusion(f32[32,8,12,2]{3,1,2,0:T(8,128)S(1)} %copy-done.3, f32[32,8,2,128]{3,1,2,0:T(8,128)S(1)} %copy-done.12, f32[32,8,2,128]{3,1,2,0:T(8,128)S(1)} %copy-done.10, f32[32,2,8,128]{3,1,2,0:T(2,128)S(1)} %copy-done.8, f32[32,4,8,128]{3,1,2,0:T(4,128)S(1)} %copy-done.5, f32[32,2,8,128]{3,1,2,0:T(2,128)S(1)} %copy.90, ...), kind=kLoop, calls=%fused_computation.12 | loop fusion | flops 7238400 | bytes 7799616 | tf_op jit(solution)/shard_map/add | solution.py:60
  98.9 2.4 %multiply_reduce_fusion.1 = (f32[32]{0:T(128)S(1)}, f32[32]{0:T(128)S(1)}, f32[32]{0:T(128)S(1)}) fusion(f32[32,6,10,130]{3,1,2,0:T(8,128)S(1)} %fusion.2, f32[32,4,8,128]{3,2,1,0:T(8,128)S(1)} %copy-done.6, f32[4,8,128]{2,0,1:T(4,128)S(1)} %copy.111, f32[4,8,128]{2,0,1:T(4,128)S(1)} %copy.110, f32[4,8,128]{2,0,1:T(4,128)S(1)} %copy-done.19, ...), kind=kLoop, calls=%fused_computation.60 | loop fusion | flops 3276704 | bytes 4292992 | tf_op jit(solution)/shard_map/reduce_sum | solution.py:72
  101.9 6.0 %all-reduce.18 = (f32[128]{0:T(128)S(1)}, f32[128]{0:T(128)S(1)}, f32[128]{0:T(128)S(1)}, f32[128]{0:T(128)S(1)}) all-reduce(f32[128]{0:T(128)S(1)} %dynamic-update-slice.12, f32[128]{0:T(128)S(1)} %dynamic-update-slice.8, f32[128]{0:T(128)S(1)} %copy-done.34, ...), channel_id=14, replica_groups=mesh['gx_0'=4,'gx_1'=2,'gy'=16,'gz'=4] {'gx_0'}, use_global_device_ids=true, to_apply=%add.12 | all-reduce | flops 512 | bytes 4096
  109.3 8.0 %all-reduce.19 = (f32[64]{0:T(128)S(1)}, f32[64]{0:T(128)S(1)}, f32[64]{0:T(128)S(1)}, f32[64]{0:T(128)S(1)}) all-reduce(f32[64]{0:T(128)S(1)} %dynamic-update-slice.13, f32[64]{0:T(128)S(1)} %dynamic-update-slice.9, f32[64]{0:T(128)S(1)} %dynamic-update-slice.1, ...), channel_id=15, replica_groups=mesh['gx_0'=4,'gx_1'=2,'gy'=16,'gz'=4] {'gx_1'}, use_global_device_ids=true, to_apply=%add.13 | all-reduce | flops 256 | bytes 2048
  118.6 28.7 %all-reduce.16 = (f32[512]{0:T(512)S(1)}, f32[512]{0:T(512)S(1)}, f32[512]{0:T(512)S(1)}, f32[512]{0:T(512)S(1)}) all-reduce(f32[512]{0:T(512)S(1)} %dynamic-update-slice.14, f32[512]{0:T(512)S(1)} %dynamic-update-slice.10, f32[512]{0:T(512)S(1)} %dynamic-update-slice.2, ...), channel_id=16, replica_groups=mesh['gx_0'=4,'gx_1'=2,'gy'=16,'gz'=4] {'gy'}, use_global_device_ids=true, to_apply=%add.14 | all-reduce | flops 2048 | bytes 16384
  148.6 7.7 %all-reduce.17 = (f32[128]{0:T(128)S(1)}, f32[128]{0:T(128)S(1)}, f32[128]{0:T(128)S(1)}, f32[128]{0:T(128)S(1)}) all-reduce(f32[128]{0:T(128)S(1)} %dynamic-update-slice.15, f32[128]{0:T(128)S(1)} %dynamic-update-slice.11, f32[128]{0:T(128)S(1)} %dynamic-update-slice.3, ...), channel_id=17, replica_groups=mesh['gx_0'=4,'gx_1'=2,'gy'=16,'gz'=4] {'gz'}, use_global_device_ids=true, to_apply=%add.15 | all-reduce | flops 512 | bytes 4096
  156.8 4.1 %multiply_subtract_fusion = f32[32,6,10,130]{3,1,2,0:T(8,128)} fusion(f32[32,6,10,130]{3,1,2,0:T(8,128)} %copy-done.1, f32[32,8,12,132]{3,1,2,0:T(8,128)S(1)} %pad_maximum_fusion, f32[32]{0:T(128)S(1)} %mul.479, f32[32]{0:T(128)S(1)} %get-tuple-element.43), kind=kLoop, calls=%fused_computation.37 | loop fusion | flops 748800 | bytes 2995456 | tf_op jit(solution)/shard_map/sub | solution.py:108
  160.9 4.8 %copy.122 = f32[32,6,10,130]{0,3,2,1:T(8,128)} copy(f32[32,6,10,130]{3,1,2,0:T(8,128)} %multiply_subtract_fusion) | data formatting | bytes 1996800 | tf_op jit(solution)/shard_map/reshape | solution.py:119
  165.8 4.8 %reshape.300 = f32[32,7800]{0,1:T(8,128)} reshape(f32[32,6,10,130]{0,3,2,1:T(8,128)} %copy.122) | data formatting | bytes 1996800 | tf_op jit(solution)/shard_map/reshape | solution.py:119
  170.6 3.0 %gather_fusion.7 = f32[256,32]{1,0:T(8,128)S(1)} fusion(f32[32,7800]{0,1:T(8,128)} %reshape.300, s32[1024]{0:T(1024)} %get-tuple-element.96), kind=kCustom, calls=%fused_computation.5.clone | custom fusion | bytes 66560 | tf_op jit(solution)/shard_map/jit(_take)/gather | solution.py:124
  173.5 3.0 %gather_fusion.6 = f32[256,32]{1,0:T(8,128)S(1)} fusion(f32[32,7800]{0,1:T(8,128)} %reshape.300, s32[1024]{0:T(1024)} %get-tuple-element.97), kind=kCustom, calls=%fused_computation.4.clone | custom fusion | bytes 66560 | tf_op jit(solution)/shard_map/jit(_take)/gather | solution.py:123
  176.5 3.0 %gather_fusion.5 = f32[256,32]{1,0:T(8,128)S(1)} fusion(f32[32,7800]{0,1:T(8,128)} %reshape.300, s32[1024]{0:T(1024)} %get-tuple-element.98), kind=kCustom, calls=%fused_computation.3.clone | custom fusion | bytes 66560 | tf_op jit(solution)/shard_map/jit(_take)/gather | solution.py:124
  179.5 3.0 %gather_fusion.4 = f32[256,32]{1,0:T(8,128)S(1)} fusion(f32[32,7800]{0,1:T(8,128)} %reshape.300, s32[1024]{0:T(1024)} %get-tuple-element.99), kind=kCustom, calls=%fused_computation.2.clone | custom fusion | bytes 66560 | tf_op jit(solution)/shard_map/jit(_take)/gather | solution.py:123
  182.5 3.0 %gather_fusion.3 = f32[256,32]{1,0:T(8,128)S(1)} fusion(f32[32,7800]{0,1:T(8,128)} %reshape.300, s32[1024]{0:T(1024)} %get-tuple-element.100), kind=kCustom, calls=%fused_computation.1.clone | custom fusion | bytes 66560 | tf_op jit(solution)/shard_map/jit(_take)/gather | solution.py:124
  185.5 3.0 %gather_fusion.2 = f32[256,32]{1,0:T(8,128)S(1)} fusion(f32[32,7800]{0,1:T(8,128)} %reshape.300, s32[1024]{0:T(1024)} %get-tuple-element.101), kind=kCustom, calls=%fused_computation.clone | custom fusion | bytes 66560 | tf_op jit(solution)/shard_map/jit(_take)/gather | solution.py:123
  190.3 19.6 %all-to-all-start = ((f32[128,1,192]{2,1,0:T(1,128)}), f32[128,1,192]{2,1,0:T(1,128)S(1)}, u32[]{:S(2)}, u32[]{:S(2)}) async-start(f32[128,1,192]{2,1,0:T(1,128)} %reshape.304), calls=%async_computation | async-start | bytes 262144 | tf_op jit(solution)/shard_map/all_to_all | solution.py:128
  209.9 18.2 %all-to-all-done = f32[128,1,192]{2,1,0:T(1,128)S(1)} async-done(((f32[128,1,192]{2,1,0:T(1,128)}), f32[128,1,192]{2,1,0:T(1,128)S(1)}, u32[]{:S(2)}, u32[]{:S(2)}) %all-to-all-start) | async-done | bytes 98336 | tf_op jit(solution)/shard_map/all_to_all | solution.py:128
  (216 shorter events, 50.5 us)
Async XLA Ops:
  0.6 231.8 %copy-start = (f32[32,128]{1,0:T(8,128)S(1)}, f32[32,128]{1,0:T(8,128)}, u32[]{:S(2)}) copy-start(f32[32,128]{1,0:T(8,128)} %param.13) | copy-start | bytes 49156
  1.4 22.8 %collective-permute-start.6 = (s32[2,8,128]{2,1,0:T(8,128)S(1)}, s32[2,8,128]{2,1,0:T(8,128)S(1)}, u32[]{:S(2)}, u32[]{:S(2)}) collective-permute-start(s32[2,8,128]{2,1,0:T(8,128)S(1)} %get-tuple-element.70), channel_id=1, source_target_pairs={{0,64},{64,128},{128,192},{192,256},{256,320},{320,384},{384,448},... | collective-permute-start | bytes 24584 | tf_op jit(solution)/shard_map/ppermute | solution.py:18
  6.0 18.2 %collective-permute-start.7 = (s32[2,8,128]{2,1,0:T(8,128)S(1)}, s32[2,8,128]{2,1,0:T(8,128)S(1)}, u32[]{:S(2)}, u32[]{:S(2)}) collective-permute-start(s32[2,8,128]{2,1,0:T(8,128)S(1)} %get-tuple-element.71), channel_id=1, source_target_pairs={{64,0},{128,64},{192,128},{256,192},{320,256},{384,320},{448,384},... | collective-permute-start | bytes 24584 | tf_op jit(solution)/shard_map/ppermute | solution.py:21
  12.5 34.1 %collective-permute-start = (f32[32,2,8,128]{3,2,1,0:T(8,128)S(1)}, f32[32,2,8,128]{3,2,1,0:T(8,128)S(1)}, u32[]{:S(2)}, u32[]{:S(2)}) collective-permute-start(f32[32,2,8,128]{3,2,1,0:T(8,128)S(1)} %get-tuple-element.51), channel_id=1, source_target_pairs={{0,64},{64,128},{128,192},{192,256},{256,320},{320,384},{384,448},... | collective-permute-start | bytes 786440 | tf_op jit(solution)/shard_map/ppermute | solution.py:18
  14.4 32.3 %collective-permute-start.1 = (f32[32,2,8,128]{3,2,1,0:T(8,128)S(1)}, f32[32,2,8,128]{3,2,1,0:T(8,128)S(1)}, u32[]{:S(2)}, u32[]{:S(2)}) collective-permute-start(f32[32,2,8,128]{3,2,1,0:T(8,128)S(1)} %get-tuple-element.52), channel_id=1, source_target_pairs={{64,0},{128,64},{192,128},{256,192},{320,256},{384,320},{448,384},... | collective-permute-start | bytes 786440 | tf_op jit(solution)/shard_map/ppermute | solution.py:21
  24.2 5.1 %collective-permute-start.8 = (s32[8,2,128]{2,1,0:T(2,128)S(1)}, s32[8,2,128]{2,1,0:T(2,128)S(1)}, u32[]{:S(2)}, u32[]{:S(2)}) collective-permute-start(s32[8,2,128]{2,1,0:T(2,128)S(1)} %get-tuple-element.68), channel_id=1, source_target_pairs={{0,4},{4,8},{8,12},{12,16},{16,20},{20,24},{24,28},{28,32},{32,36}... | collective-permute-start | bytes 24584 | tf_op jit(solution)/shard_map/ppermute | solution.py:18
  25.5 4.5 %collective-permute-start.9 = (s32[8,2,128]{2,1,0:T(2,128)S(1)}, s32[8,2,128]{2,1,0:T(2,128)S(1)}, u32[]{:S(2)}, u32[]{:S(2)}) collective-permute-start(s32[8,2,128]{2,1,0:T(2,128)S(1)} %get-tuple-element.69), channel_id=1, source_target_pairs={{4,0},{8,4},{12,8},{16,12},{20,16},{24,20},{28,24},{32,28},{36,32}... | collective-permute-start | bytes 24584 | tf_op jit(solution)/shard_map/ppermute | solution.py:21
  28.0 34.2 %copy-start.4 = (f32[32,4,8,128]{3,1,2,0:T(4,128)}, f32[32,4,8,128]{3,1,2,0:T(4,128)S(1)}, u32[]{:S(2)}) copy-start(f32[32,4,8,128]{3,1,2,0:T(4,128)S(1)} %copy.105) | copy-start | bytes 1572868
  30.1 11.1 %collective-permute-start.10 = (s32[8,12,2]{2,1,0:T(8,128)S(1)}, s32[8,12,2]{2,1,0:T(8,128)S(1)}, u32[]{:S(2)}, u32[]{:S(2)}) collective-permute-start(s32[8,12,2]{2,1,0:T(8,128)S(1)} %get-tuple-element.66), channel_id=1, source_target_pairs={{0,1},{1,2},{2,3},{4,5},{5,6},{6,7},{8,9},{9,10},{10,11},{12,13},{... | collective-permute-start | bytes 2312 | tf_op jit(solution)/shard_map/ppermute | solution.py:18
  33.2 7.9 %collective-permute-start.11 = (s32[8,12,2]{2,1,0:T(8,128)S(1)}, s32[8,12,2]{2,1,0:T(8,128)S(1)}, u32[]{:S(2)}, u32[]{:S(2)}) collective-permute-start(s32[8,12,2]{2,1,0:T(8,128)S(1)} %get-tuple-element.67), channel_id=1, source_target_pairs={{1,0},{2,1},{3,2},{5,4},{6,5},{7,6},{9,8},{10,9},{11,10},{13,12},{... | collective-permute-start | bytes 2312 | tf_op jit(solution)/shard_map/ppermute | solution.py:21
  46.9 16.4 %copy-start.7 = (f32[32,2,8,128]{3,1,2,0:T(2,128)}, f32[32,2,8,128]{3,1,2,0:T(2,128)S(1)}, u32[]{:S(2)}) copy-start(f32[32,2,8,128]{3,1,2,0:T(2,128)S(1)} %copy.92) | copy-start | bytes 786436
  47.1 9.5 %collective-permute-start.2 = (f32[32,8,2,128]{3,1,2,0:T(8,128)S(1)}, f32[32,8,2,128]{3,1,2,0:T(8,128)S(1)}, u32[]{:S(2)}, u32[]{:S(2)}) collective-permute-start(f32[32,8,2,128]{3,1,2,0:T(8,128)S(1)} %get-tuple-element.49), channel_id=1, source_target_pairs={{0,4},{4,8},{8,12},{12,16},{16,20},{20,24},{24,28},{28,32},{32,36}... | collective-permute-start | bytes 786440 | tf_op jit(solution)/shard_map/ppermute | solution.py:18
  50.7 11.6 %collective-permute-start.3 = (f32[32,8,2,128]{3,1,2,0:T(8,128)S(1)}, f32[32,8,2,128]{3,1,2,0:T(8,128)S(1)}, u32[]{:S(2)}, u32[]{:S(2)}) collective-permute-start(f32[32,8,2,128]{3,1,2,0:T(8,128)S(1)} %get-tuple-element.50), channel_id=1, source_target_pairs={{4,0},{8,4},{12,8},{16,12},{20,16},{24,20},{28,24},{32,28},{36,32}... | collective-permute-start | bytes 786440 | tf_op jit(solution)/shard_map/ppermute | solution.py:21
  65.0 9.5 %copy-start.25 = (f32[4,8,128]{2,1,0:T(8,128)S(1)}, f32[4,8,128]{2,1,0:T(8,128)}, u32[]{:S(2)}) copy-start(f32[4,8,128]{2,1,0:T(8,128)} %get-tuple-element.58) | copy-start | bytes 49156
  65.0 9.5 %copy-start.24 = (f32[4,8,128]{2,1,0:T(8,128)S(1)}, f32[4,8,128]{2,1,0:T(8,128)}, u32[]{:S(2)}) copy-start(f32[4,8,128]{2,1,0:T(8,128)} %get-tuple-element.53) | copy-start | bytes 49156
  65.0 10.1 %copy-start.23 = (f32[4,8,128]{2,1,0:T(8,128)S(1)}, f32[4,8,128]{2,1,0:T(8,128)}, u32[]{:S(2)}) copy-start(f32[4,8,128]{2,1,0:T(8,128)} %get-tuple-element.54) | copy-start | bytes 49156
  65.0 10.7 %copy-start.22 = (f32[4,8,128]{2,1,0:T(8,128)S(1)}, f32[4,8,128]{2,1,0:T(8,128)}, u32[]{:S(2)}) copy-start(f32[4,8,128]{2,1,0:T(8,128)} %get-tuple-element.55) | copy-start | bytes 49156
  68.1 14.6 %collective-permute-start.5 = (f32[32,8,12,2]{0,1,3,2:T(8,128)S(1)}, f32[32,8,12,2]{0,1,3,2:T(8,128)S(1)}, u32[]{:S(2)}, u32[]{:S(2)}) collective-permute-start(f32[32,8,12,2]{0,1,3,2:T(8,128)S(1)} %copy.94), channel_id=1, source_target_pairs={{1,0},{2,1},{3,2},{5,4},{6,5},{7,6},{9,8},{10,9},{11,10},{13,12},{... | collective-permute-start | bytes 73736 | tf_op jit(solution)/shard_map/ppermute | solution.py:21
  69.4 11.0 %collective-permute-start.4 = (f32[32,8,12,2]{0,1,3,2:T(8,128)S(1)}, f32[32,8,12,2]{0,1,3,2:T(8,128)S(1)}, u32[]{:S(2)}, u32[]{:S(2)}) collective-permute-start(f32[32,8,12,2]{0,1,3,2:T(8,128)S(1)} %copy.93), channel_id=1, source_target_pairs={{0,1},{1,2},{2,3},{4,5},{5,6},{6,7},{8,9},{9,10},{10,11},{12,13},{... | collective-permute-start | bytes 73736 | tf_op jit(solution)/shard_map/ppermute | solution.py:18
  90.1 8.8 %copy-start.6 = (f32[32,4,8,128]{3,2,1,0:T(8,128)S(1)}, f32[32,4,8,128]{3,2,1,0:T(8,128)}, u32[]{:S(2)}) copy-start(f32[32,4,8,128]{3,2,1,0:T(8,128)} %param.8) | copy-start | bytes 1572868
  90.1 8.8 %copy-start.18 = (f32[4,8,128]{2,0,1:T(4,128)S(1)}, f32[4,8,128]{2,0,1:T(4,128)}, u32[]{:S(2)}) copy-start(f32[4,8,128]{2,0,1:T(4,128)} %copy.106) | copy-start | bytes 49156
  90.1 8.8 %copy-start.19 = (f32[4,8,128]{2,0,1:T(4,128)S(1)}, f32[4,8,128]{2,0,1:T(4,128)}, u32[]{:S(2)}) copy-start(f32[4,8,128]{2,0,1:T(4,128)} %copy.109) | copy-start | bytes 49156
  90.1 8.8 %copy-start.20 = (f32[4,8,128]{2,0,1:T(4,128)S(1)}, f32[4,8,128]{2,0,1:T(4,128)}, u32[]{:S(2)}) copy-start(f32[4,8,128]{2,0,1:T(4,128)} %copy.108) | copy-start | bytes 49156
  165.8 22.8 %copy-start.26 = (f32[256]{0:T(256)S(1)}, f32[256]{0:T(256)}, u32[]{:S(2)}) copy-start(f32[256]{0:T(256)} %select_multiply_fusion) | copy-start | bytes 3076
  165.8 22.8 %copy-start.27 = (pred[256]{0:T(512)(128)(4,1)S(1)}, pred[256]{0:T(512)(128)(4,1)}, u32[]{:S(2)}) copy-start(pred[256]{0:T(512)(128)(4,1)} %get-tuple-element.75) | copy-start | bytes 772
  165.8 22.8 %copy-start.28 = (pred[256]{0:T(512)(128)(4,1)S(1)}, pred[256]{0:T(512)(128)(4,1)}, u32[]{:S(2)}) copy-start(pred[256]{0:T(512)(128)(4,1)} %get-tuple-element.76) | copy-start | bytes 772
  165.8 22.8 %copy-start.29 = (pred[256]{0:T(512)(128)(4,1)S(1)}, pred[256]{0:T(512)(128)(4,1)}, u32[]{:S(2)}) copy-start(pred[256]{0:T(512)(128)(4,1)} %get-tuple-element.77) | copy-start | bytes 772
  165.8 22.8 %copy-start.30 = (pred[256]{0:T(512)(128)(4,1)S(1)}, pred[256]{0:T(512)(128)(4,1)}, u32[]{:S(2)}) copy-start(pred[256]{0:T(512)(128)(4,1)} %get-tuple-element.78) | copy-start | bytes 772
  165.8 22.8 %copy-start.31 = (pred[256]{0:T(512)(128)(4,1)S(1)}, pred[256]{0:T(512)(128)(4,1)}, u32[]{:S(2)}) copy-start(pred[256]{0:T(512)(128)(4,1)} %get-tuple-element.79) | copy-start | bytes 772
  165.8 22.8 %copy-start.32 = (pred[256]{0:T(512)(128)(4,1)S(1)}, pred[256]{0:T(512)(128)(4,1)}, u32[]{:S(2)}) copy-start(pred[256]{0:T(512)(128)(4,1)} %get-tuple-element.41) | copy-start | bytes 772
  173.5 36.3 %copy-start.35 = (s32[128]{0:T(128)S(1)}, s32[128]{0:T(128)}, u32[]{:S(2)}) copy-start(s32[128]{0:T(128)} %param.12) | copy-start | bytes 1540
  190.3 37.8 %all-to-all-start = ((f32[128,1,192]{2,1,0:T(1,128)}), f32[128,1,192]{2,1,0:T(1,128)S(1)}, u32[]{:S(2)}, u32[]{:S(2)}) async-start(f32[128,1,192]{2,1,0:T(1,128)} %reshape.304), calls=%async_computation | async-start | bytes 262144 | tf_op jit(solution)/shard_map/all_to_all | solution.py:128
  (17 other events, 74.1 us)
